TPU v7x, 32 devices: a whole 2x2x4 slice. The times are simulated.
32 devices in a mesh: mode: 8 (over z, y), row: 4 (over x, core).
Axes of the slice: x: 2, y: 2, z: 4, core: 2. Of those that a mesh axis runs over, the one named last changes fastest.
Arguments:
- density: float32 [2, 2048, 2048], P(None, 'row', 'mode'), may hold values from -6 to 6
- auxiliary: float32 [2048, 32, 2, 128], P('row', 'mode'), may hold values from -2 to 2
- hamiltonian: bfloat16 [2048, 2048], P('row'), as said below
- coupling: int32 [2, 128], replicated, may hold values from 0 to 2047, as said below
- lead_index: int32 [32], P('mode'), may hold values from 0 to 1
- mode_level: float32 [32], P('mode'), may hold values from -2 to 2
- mode_width: float32 [32], P('mode'), may hold values from 0.05 to 3
- residue: float32 [32, 2], P('mode'), may hold values from -4 to 4
- occupation: float32 [32], P('mode'), may hold values from 0 to 1
- lead_gamma: bfloat16 [2, 128, 128], replicated, may hold values from -0.5 to 0.5
Outputs:
- density_rate: float32 [2, 2048, 2048], P(None, 'row', 'mode')
- auxiliary_rate: float32 [2048, 32, 2, 128], P('row', 'mode')
Inputs may be any that keep to these rules, and one draw needn't show every extreme that they name: `coupling`: all 256 entries are distinct orbitals. `hamiltonian`: Symmetric.
All inputs are finite; a program needn't handle non-finite values.
Results may differ from a plain program's by a relative error of at most 0.0044.
Values may be sent and summed in bfloat16 or wider, within the bound.
A program may use at most 128 MiB of HBM per device.

v0:
```python
import jax
import jax.numpy as jnp
from jax import lax
from jax.sharding import PartitionSpec as P

step_size = 0.1
highest = lax.Precision.HIGHEST


def shards(
    density,
    auxiliary,
    hamiltonian,
    coupling,
    lead_index,
    mode_level,
    mode_width,
    residue,
    occupation,
    lead_gamma,
):
    panel_rows = density.shape[1]
    columns = density.shape[2]
    lead_count = coupling.shape[0]
    coupled = coupling.shape[1]
    local_modes = auxiliary.shape[1]
    row_start = lax.axis_index("row") * panel_rows
    col_start = lax.axis_index("mode") * columns
    flat_coupling = coupling.reshape(-1)
    own_columns = lax.dynamic_slice_in_dim(hamiltonian, col_start, columns, 1)
    ham_columns = lax.all_gather(own_columns, "row", axis=0, tiled=True)
    row_select = (
        row_start + jnp.arange(panel_rows, dtype=jnp.int32)[:, None] == flat_coupling[None, :]
    ).astype(jnp.float32)
    col_select = (
        col_start + jnp.arange(columns, dtype=jnp.int32)[:, None] == flat_coupling[None, :]
    ).astype(jnp.float32)
    lead_onehot = (lead_index[:, None] == jnp.arange(lead_count, dtype=jnp.int32)[None, :]).astype(
        jnp.float32
    )
    row_select_b = row_select.astype(jnp.bfloat16)
    gamma_rows = jnp.stack(
        [
            jnp.dot(
                row_select_b[:, lead_pos * coupled : (lead_pos + 1) * coupled],
                lead_gamma[lead_pos],
                preferred_element_type=jnp.float32,
            )
            for lead_pos in range(lead_count)
        ],
        axis=1,
    )

    def rates(state_rho, state_aux):
        dens_b = state_rho.astype(jnp.bfloat16)
        aux_b = state_aux.astype(jnp.bfloat16).reshape(panel_rows, -1)
        ham_aux = jnp.dot(
            hamiltonian,
            lax.all_gather(aux_b, "row", axis=0, tiled=True),
            preferred_element_type=jnp.float32,
        )
        col_block = lax.all_gather(dens_b, "row", axis=1, tiled=True)
        ham_rho = jnp.einsum(
            "an,cnt->cat", hamiltonian, col_block, preferred_element_type=jnp.float32
        )
        row_panel = lax.all_gather(dens_b, "mode", axis=2, tiled=True).reshape(2 * panel_rows, -1)
        rho_ham = jnp.dot(row_panel, ham_columns, preferred_element_type=jnp.float32).reshape(
            2, panel_rows, columns
        )
        all_select = (
            jnp.arange(row_panel.shape[1], dtype=jnp.int32)[:, None] == flat_coupling[None, :]
        ).astype(jnp.bfloat16)
        coupled_rho = jnp.dot(row_panel, all_select, preferred_element_type=jnp.float32)
        coupled_rho = coupled_rho.astype(jnp.bfloat16).reshape(2, panel_rows, lead_count, coupled)
        sources = jnp.stack(
            [
                jnp.dot(
                    coupled_rho[:, :, lead_pos, :].reshape(2 * panel_rows, coupled),
                    lead_gamma[lead_pos],
                    preferred_element_type=jnp.float32,
                ).reshape(2, panel_rows, coupled)
                for lead_pos in range(lead_count)
            ],
            axis=2,
        )
        partial_sums = jnp.einsum(
            "akcj,kl->aclj", state_aux, lead_onehot, precision=highest
        ).reshape(panel_rows, 2 * lead_count * coupled)
        panel_sums = lax.psum(partial_sums, "mode")
        full_sums = lax.all_gather(panel_sums, "row", axis=0, tiled=True).reshape(
            -1, 2, lead_count * coupled
        )
        own_sums = lax.dynamic_slice_in_dim(full_sums, row_start, panel_rows, 0)
        cross_sums = lax.dynamic_slice_in_dim(full_sums, col_start, columns, 0)
        forward = jnp.einsum("acj,tj->cat", own_sums, col_select, precision=highest)
        backward = jnp.einsum("aj,tcj->cat", row_select, cross_sums, precision=highest)
        commutator = ham_rho - rho_ham
        rho_rate = jnp.stack(
            [commutator[1] + forward[0] + backward[0], -commutator[0] + forward[1] - backward[1]]
        )
        ham_aux = ham_aux.reshape(panel_rows, local_modes, 2, coupled)
        source_rows = sources.transpose(1, 2, 0, 3)
        driven = jnp.zeros_like(state_aux)
        for lead_pos in range(lead_count):
            weight_pos = lead_onehot[:, lead_pos][None, :, None, None]
            lead_term = source_rows[:, lead_pos][:, None, :, :]
            gamma_term = gamma_rows[:, lead_pos][:, None, None, :]
            driven = (
                driven
                + weight_pos * lead_term
                - weight_pos * occupation[None, :, None, None] * gamma_term
            )
        shifted = ham_aux - mode_level[None, :, None, None] * state_aux
        decay = mode_width[None, :, None]
        res_re = residue[:, 0][None, :, None]
        res_im = residue[:, 1][None, :, None]
        aux_re = (
            shifted[:, :, 1, :]
            - decay * state_aux[:, :, 0, :]
            + res_re * driven[:, :, 0, :]
            - res_im * driven[:, :, 1, :]
        )
        aux_im = (
            -shifted[:, :, 0, :]
            - decay * state_aux[:, :, 1, :]
            + res_re * driven[:, :, 1, :]
            + res_im * driven[:, :, 0, :]
        )
        return (rho_rate, jnp.stack([aux_re, aux_im], axis=2))

    first_rho, first_aux = rates(density, auxiliary)
    middle_rho = density + 0.5 * step_size * first_rho
    middle_aux = auxiliary + 0.5 * step_size * first_aux
    second_rho, second_aux = rates(middle_rho, middle_aux)
    return (first_rho + 2.0 * second_rho, first_aux + 2.0 * second_aux)


def solution(mesh):
    in_specs = (
        P(None, "row", "mode"),
        P("row", "mode", None, None),
        P("row", None),
        P(),
        P("mode"),
        P("mode"),
        P("mode"),
        P("mode", None),
        P("mode"),
        P(),
    )
    out_specs = (P(None, "row", "mode"), P("row", "mode", None, None))
    return jax.shard_map(shards, mesh=mesh, in_specs=in_specs, out_specs=out_specs, check_vma=False)
```

profile of v0, /device:TPU:0, one launch (start us, length us, event | category | flops | bytes accessed | tf_op | source)
XLA Modules:
  0.0 540.4 jit_solution(8981585179444016876)
XLA Ops:
  7.2 2.5 convert_element_type.35
  11.3 1.6 copy.28
  14.0 4.8 fusion.11
  18.8 2.8 copy.57
  23.6 25.0 %all-gather.22.cloned.1.call-done = bf16[2048,1024]{1,0:T(8,128)(2,1)} async-done(((bf16[512,1024]{1,0:T(8,128)(2,1)}), bf16[2048,1024]{1,0:T(8,128)(2,1)}) %all-gather.22.cloned.1.call-update) | async-done | bytes 4194320 | tf_op jit(solution)/shard_map/all_gather | solution.py:59
  48.6 5.8 %fusion.94 = f32[512,1024]{1,0:T(8,128)} fusion(bf16[512,2048]{1,0:T(8,128)(2,1)S(1)} %copy-done, bf16[2048,1024]{1,0:T(8,128)(2,1)} %all-gather.22.cloned.1.call-done), kind=kOutput, calls=%fused_computation.140 | convolution fusion | flops 2147483648 | bytes 8388608 | tf_op jit(solution)/shard_map/dot_general | solution.py:57
  54.4 4.0 reshape.113
  58.5 4.9 multiply_subtract_fusion.1
  63.4 60.2 %all-gather.14.cloned.1.call-done = bf16[2,512,2048]{1,2,0:T(8,128)(2,1)} async-done(((bf16[2,512,256]{1,2,0:T(8,128)(2,1)}), bf16[2,512,2048]{1,2,0:T(8,128)(2,1)}) %all-gather.14.cloned.1.call-update) | async-done | bytes 4194320 | tf_op jit(solution)/shard_map/all_gather | solution.py:66
  123.6 6.3 %copy.29 = bf16[2,512,2048]{2,1,0:T(8,128)(2,1)} copy(bf16[2,512,2048]{1,2,0:T(8,128)(2,1)} %all-gather.14.cloned.1.call-done) | data formatting | bytes 8388608 | tf_op jit(solution)/shard_map/all_gather | solution.py:66
  129.9 4.3 fusion.30
  134.2 2.2 reshape.114
  136.5 2.2 fusion.93
  144.5 2.2 add_subtract_fusion.1
  146.8 5.4 %fusion.39 = (f32[512,4,1,128]{3,2,1,0:T(1,128)S(1)}, f32[512,4,1,128]{3,2,1,0:T(1,128)S(1)}) fusion(f32[512,4,2,128]{3,2,1,0:T(2,128)S(1)} %copy-done.11, f32[512,4,2,128]{3,2,1,0:T(2,128)S(1)} %copy-done.1, f32[512,4,2,128]{3,2,1,0:T(2,128)S(1)} %add_subtract_fusion.1, f32[4]{0:T(128)S(1)} %get-tuple-element.29, f32[4]{0:T(128)S(1)} %get-tuple-element.28, ...), kind=kLoop, calls=%fused_computation.49 | loop fusion | flops 3407872 | bytes 8388656 | tf_op jit(solution)/shard_map/sub | solution.py:118
  152.2 4.0 fusion.91
  157.5 3.3 fusion.14
  160.8 2.3 copy.58
  164.6 99.6 %all-reduce.3.cloned.1.call-done = (f32[512,512]{0,1:T(8,128)}, f32[512,512]{0,1:T(8,128)}) async-done(((f32[512,512]{0,1:T(8,128)}, f32[512,512]{0,1:T(8,128)}), (f32[512,512]{0,1:T(8,128)}, f32[512,512]{0,1:T(8,128)})) %all-reduce.3.cloned.1.call-update) | async-done | bytes 2097168 | tf_op jit(solution)/shard_map/psum | solution.py:89
  264.2 2.6 reshape.117
  267.7 14.0 %all-gather.12.cloned.1.call-done = bf16[2048,256]{1,0:T(8,128)(2,1)} async-done(((bf16[512,256]{1,0:T(8,128)(2,1)}), bf16[2048,256]{1,0:T(8,128)(2,1)}) %all-gather.12.cloned.1.call-update) | async-done | bytes 1048592 | tf_op jit(solution)/shard_map/all_gather | solution.py:31
  281.6 4.8 convolution_bitcast_fusion.4
  286.4 2.6 copy.30
  289.0 2.6 copy.31
  291.6 14.1 %all-gather.10.cloned.1.call-done = bf16[2,2048,256]{1,2,0:T(8,128)(2,1)} async-done(((bf16[2,512,256]{1,2,0:T(8,128)(2,1)}), bf16[2,2048,256]{1,2,0:T(8,128)(2,1)}) %all-gather.10.cloned.1.call-update) | async-done | bytes 2097168 | tf_op jit(solution)/shard_map/all_gather | solution.py:62
  305.6 4.1 fusion.26
  309.7 31.8 %all-gather.16.cloned.1.call-done = f32[2048,512]{0,1:T(8,128)} async-done(((f32[512,512]{0,1:T(8,128)}), f32[2048,512]{0,1:T(8,128)}) %all-gather.16.cloned.1.call-update) | async-done | bytes 4194320 | tf_op jit(solution)/shard_map/all_gather | solution.py:90
  341.5 2.0 convolution_bitcast_fusion.3
  343.6 2.1 convolution_bitcast_fusion.2
  348.7 28.9 %all-gather.26.cloned.1.call-done = bf16[2048,1024]{1,0:T(8,128)(2,1)} async-done(((bf16[512,1024]{1,0:T(8,128)(2,1)}), bf16[2048,1024]{1,0:T(8,128)(2,1)}) %all-gather.26.cloned.1.call-update) | async-done | bytes 4194320 | tf_op jit(solution)/shard_map/all_gather | solution.py:59
  377.6 5.9 %fusion.95 = f32[1024,512]{1,0:T(8,128)} fusion(bf16[2048,1024]{1,0:T(8,128)(2,1)} %all-gather.26.cloned.1.call-done, bf16[512,2048]{1,0:T(8,128)(2,1)S(1)} %copy-done), kind=kOutput, calls=%fused_computation.141 | convolution fusion | flops 2147483648 | bytes 8388608 | tf_op jit(solution)/shard_map/dot_general | solution.py:57
  383.4 4.4 copy.47
  387.8 4.9 multiply_subtract_fusion
  392.7 20.9 %all-gather.24.cloned.1.call-done = f32[2048,512]{0,1:T(8,128)} async-done(((f32[512,512]{0,1:T(8,128)}), f32[2048,512]{0,1:T(8,128)}) %all-gather.24.cloned.1.call-update) | async-done | bytes 4194320 | tf_op jit(solution)/shard_map/all_gather | solution.py:90
  413.6 2.9 convolution_bitcast_fusion.1
  416.6 3.1 convolution_bitcast_fusion
  419.7 69.0 %all-gather.20.cloned.1.call-done = bf16[2,512,2048]{1,2,0:T(8,128)(2,1)} async-done(((bf16[2,512,256]{1,2,0:T(8,128)(2,1)}), bf16[2,512,2048]{1,2,0:T(8,128)(2,1)}) %all-gather.20.cloned.1.call-update) | async-done | bytes 4194320 | tf_op jit(solution)/shard_map/all_gather | solution.py:66
  488.6 6.3 %copy.48 = bf16[2,512,2048]{2,1,0:T(8,128)(2,1)} copy(bf16[2,512,2048]{1,2,0:T(8,128)(2,1)} %all-gather.20.cloned.1.call-done) | data formatting | bytes 8388608 | tf_op jit(solution)/shard_map/all_gather | solution.py:66
  495.0 4.8 fusion.29
  499.7 2.0 reshape.120
  501.7 2.1 fusion.92
  507.0 2.3 fusion.41
  509.4 1.8 all-gather.18.cloned.1.call-done
  511.2 3.3 fusion.23
  517.0 2.5 copy.53
  519.5 3.5 add_subtract_fusion
  523.0 5.7 %multiply_subtract_fusion.2 = (f32[512,4,1,128]{3,2,1,0:T(1,128)S(1)}, f32[512,4,1,128]{3,2,1,0:T(1,128)S(1)}) fusion(f32[512,4,2,128]{3,2,1,0:T(2,128)S(1)} %copy-done.3, f32[512,4,2,128]{3,2,1,0:T(2,128)S(1)} %copy-done.10, f32[512,4,2,128]{3,2,1,0:T(2,128)S(1)} %add_subtract_fusion, f32[4]{0:T(128)S(1)} %get-tuple-element.29, f32[4]{0:T(128)S(1)} %get-tuple-element.28, ...), kind=kLoop, calls=%fused_computation.58 | loop fusion | flops 3407872 | bytes 8388656 | tf_op jit(solution)/shard_map/sub | solution.py:118
  528.7 4.6 fusion
  (107 shorter events, 22.6 us)
Async XLA Ops:
  7.2 41.4 %copy-start = (bf16[512,2048]{1,0:T(8,128)(2,1)S(1)}, bf16[512,2048]{1,0:T(8,128)(2,1)}, u32[]{:S(2)}) copy-start(bf16[512,2048]{1,0:T(8,128)(2,1)} %param.12) | copy-start | bytes 6291460
  7.2 41.4 %all-gather.22.cloned.1.call-start = ((), (), s32[]{:S(2)}) async-start(), calls=%async_computation.6 | async-start | bytes 5242880 | tf_op jit(solution)/shard_map/all_gather | solution.py:59
  11.3 2.7 copy-start.24
  11.3 112.3 %all-gather.14.cloned.1.call-start = ((), (), s32[]{:S(2)}) async-start(), calls=%async_computation.2 | async-start | bytes 4718592 | tf_op jit(solution)/shard_map/all_gather | solution.py:66
  12.9 5.9 %copy-start.6 = (f32[2,512,256]{1,2,0:T(8,128)}, f32[2,512,256]{1,2,0:T(8,128)S(1)}, u32[]{:S(2)}) copy-start(f32[2,512,256]{1,2,0:T(8,128)S(1)} %copy.28) | copy-start | bytes 3145732
  13.9 250.3 %all-reduce.3.cloned.1.call-start = ((), (), s32[]{:S(2)}) async-start(), calls=%async_computation.9 | async-start | bytes 4194304 | tf_op jit(solution)/shard_map/psum | solution.py:89
  13.9 7.7 %copy-start.25 = (f32[4,2]{0,1:T(2,128)S(1)}, f32[4,2]{0,1:T(2,128)}, u32[]{:S(2)}) copy-start(f32[4,2]{0,1:T(2,128)} %param.17) | copy-start | bytes 100
  13.9 7.7 %copy-start.26 = (f32[4]{0:T(128)S(1)}, f32[4]{0:T(128)}, u32[]{:S(2)}) copy-start(f32[4]{0:T(128)} %param.18) | copy-start | bytes 52
  13.9 7.7 %copy-start.21 = (s32[2,128]{1,0:T(2,128)S(1)}, s32[2,128]{1,0:T(2,128)}, u32[]{:S(2)}) copy-start(s32[2,128]{1,0:T(2,128)} %param.13) | copy-start | bytes 3076
  14.0 7.9 %copy-start.20 = (bf16[2,128,128]{2,1,0:T(8,128)(2,1)S(1)}, bf16[2,128,128]{2,1,0:T(8,128)(2,1)}, u32[]{:S(2)}) copy-start(bf16[2,128,128]{2,1,0:T(8,128)(2,1)} %param.19) | copy-start | bytes 196612
  23.6 120.6 %copy-start.8 = (f32[512,4,128]{2,1,0:T(4,128)}, f32[512,4,128]{2,1,0:T(4,128)S(1)}, u32[]{:S(2)}) copy-start(f32[512,4,128]{2,1,0:T(4,128)S(1)} %get-tuple-element.32) | copy-start | bytes 3145732
  54.4 4.0 copy-start.22
  143.3 1.2 copy-start.9
  144.5 2.2 copy-start.1
  144.5 2.3 copy-start.11
  144.5 2.3 copy-start.23
  152.2 4.0 copy-start.4
  156.2 1.3 copy-start.2
  163.2 118.5 %all-gather.12.cloned.1.call-start = ((), (), s32[]{:S(2)}) async-start(), calls=%async_computation.1 | async-start | bytes 1310720 | tf_op jit(solution)/shard_map/all_gather | solution.py:31
  164.0 141.7 %all-gather.10.cloned.1.call-start = ((), (), s32[]{:S(2)}) async-start(), calls=%async_computation | async-start | bytes 2621440 | tf_op jit(solution)/shard_map/all_gather | solution.py:62
  164.6 177.0 %all-gather.16.cloned.1.call-start = ((), (), s32[]{:S(2)}) async-start(), calls=%async_computation.3 | async-start | bytes 5242880 | tf_op jit(solution)/shard_map/all_gather | solution.py:90
  264.2 113.4 %all-gather.26.cloned.1.call-start = ((), (), s32[]{:S(2)}) async-start(), calls=%async_computation.8 | async-start | bytes 5242880 | tf_op jit(solution)/shard_map/all_gather | solution.py:59
  266.8 146.8 %all-gather.24.cloned.1.call-start = ((), (), s32[]{:S(2)}) async-start(), calls=%async_computation.7 | async-start | bytes 5242880 | tf_op jit(solution)/shard_map/all_gather | solution.py:90
  267.6 221.0 %all-gather.20.cloned.1.call-start = ((), (), s32[]{:S(2)}) async-start(), calls=%async_computation.5 | async-start | bytes 4718592 | tf_op jit(solution)/shard_map/all_gather | solution.py:66
  341.5 4.2 copy-start.19
  345.7 1.3 copy-start.7
  346.1 0.8 copy-start.12
  346.1 1.0 copy-start.14
  348.1 163.1 %all-gather.18.cloned.1.call-start = ((), (), s32[]{:S(2)}) async-start(), calls=%async_computation.4 | async-start | bytes 2621440 | tf_op jit(solution)/shard_map/all_gather | solution.py:62
  504.3 2.7 copy-start.27
  504.4 2.7 copy-start.16
  511.2 3.3 copy-start.17
  511.2 3.3 copy-start.18
  514.5 1.0 copy-start.13
  514.5 1.2 copy-start.15
  519.5 3.5 copy-start.3
  519.5 3.5 copy-start.10
  523.0 5.7 %copy-start.5 = (f32[512,4,1,128]{3,2,1,0:T(1,128)S(1)}, f32[512,4,1,128]{3,2,1,0:T(1,128)}, u32[]{:S(2)}) copy-start(f32[512,4,1,128]{3,2,1,0:T(1,128)} %copy-done.4) | copy-start | bytes 3145732
Sparse Core Ops, SparseCore 0:
  11.4 37.1 all-gather.21
  50.8 72.7 all-gather.13
  163.3 100.8 all-reduce.2
  265.6 15.9 all-gather.11
  283.0 22.5 all-gather.9
  307.0 34.4 all-gather.15
  343.1 34.4 all-gather.25
  379.1 34.4 all-gather.23
  415.8 72.7 all-gather.19
  490.0 21.0 all-gather.17
where the time goes:
time: 545 us; the launch traced here: 540 us
  waiting for transfers between devices  367 us (67%)
  local copies, waits for them, and re-layouts  58.1 us (11%)
  matrix products  55.6 us (10%)
  other arithmetic  44.4 us (8%)
  between operations  14.9 us (3%)
    all_gather x2, waiting for transfers between devices, rates(): lax.all_gather(dens_b, 'mode', axis=2, tiled=True)  129 us
    psum x1, waiting for transfers between devices, rates(): panel_sums = lax.psum(partial_sums, 'mode')  99.6 us
    all_gather x2, waiting for transfers between devices, rates(): lax.all_gather(aux_b, 'row', axis=0, tiled=True)  53.9 us
    all_gather x2, waiting for transfers between devices, rates(): lax.all_gather(panel_sums, 'row', axis=0, tiled=True)  52.7 us
    all_gather x2, waiting for transfers between devices, rates(): col_block = lax.all_gather(dens_b, 'row', axis=1, tiled=True)  15.9 us
    all_gather x1, waiting for transfers between devices, shards(): ham_columns = lax.all_gather(own_columns, 'row', axis=0, tiled=True)  14 us
    all_gather x2, local copies, waits for them, and re-layouts, rates(): lax.all_gather(dens_b, 'mode', axis=2, tiled=True)  12.7 us
    dot_general x2, matrix products, rates(): jnp.dot(hamiltonian, lax.all_gather(aux_b, 'row', axis=0, tiled=True), pr...  11.7 us
  transfers between devices with their start and end apart: 10, of which 10 were waited for; matrix products, arithmetic and copies ran while one was open for 17% of the time, Pallas kernels for 0%

commit v1 on v0

--- a/solution.py
+++ b/solution.py
@@ -86,7 +86,7 @@
         partial_sums = jnp.einsum(
             "akcj,kl->aclj", state_aux, lead_onehot, precision=highest
         ).reshape(panel_rows, 2 * lead_count * coupled)
-        panel_sums = lax.psum(partial_sums, "mode")
+        panel_sums = jnp.sum(lax.all_gather(partial_sums, "mode"), axis=0)
         full_sums = lax.all_gather(panel_sums, "row", axis=0, tiled=True).reshape(
             -1, 2, lead_count * coupled
         )

time: 545 us -> 685 us (1.26)
  waiting for transfers between devices: 367 us -> 495 us
  other arithmetic: 44.4 us -> 55.4 us
    all_gather x0 -> x2, waiting for transfers between devices: none -> 243 us  [rates(): panel_sums = jnp.sum(lax.all_gather(partial_sums, 'mode'), axis=0)]
    psum x1 -> x0, waiting for transfers between devices: 99.6 us -> none  [rates(): panel_sums = lax.psum(partial_sums, 'mode')]
    all_gather x2, waiting for transfers between devices: 129 us -> 116 us  [rates(): lax.all_gather(dens_b, 'mode', axis=2, tiled=True)]
    reduce_sum x0 -> x2, other arithmetic: none -> 10.9 us  [rates(): panel_sums = jnp.sum(lax.all_gather(partial_sums, 'mode'), axis=0)]
    all_gather x0 -> x2, local copies, waits for them, and re-layouts: none -> 10.8 us  [rates(): lax.all_gather(panel_sums, 'row', axis=0, tiled=True)]
    all_gather x2, waiting for transfers between devices: 15.9 us -> 25.6 us  [rates(): col_block = lax.all_gather(dens_b, 'row', axis=1, tiled=True)]
    all_gather x2, waiting for transfers between devices: 52.7 us -> 43.9 us  [rates(): lax.all_gather(panel_sums, 'row', axis=0, tiled=True)]
  transfers between devices with their start and end apart: 10 -> 11, of which waited for: 10 -> 11; matrix products, arithmetic and copies ran while one was open for 17% -> 16% of each run, Pallas kernels for 0% -> 0%
where the time goes in v1:
time: 685 us; the launch traced here: 679 us
  waiting for transfers between devices  495 us (72%)
  local copies, waits for them, and re-layouts  60.5 us (9%)
  other arithmetic  55.4 us (8%)
  matrix products  52.6 us (8%)
  between operations  14.8 us (2%)
    all_gather x2, waiting for transfers between devices, rates(): panel_sums = jnp.sum(lax.all_gather(partial_sums, 'mode'), axis=0)  243 us
    all_gather x2, waiting for transfers between devices, rates(): lax.all_gather(dens_b, 'mode', axis=2, tiled=True)  116 us
    all_gather x2, waiting for transfers between devices, rates(): lax.all_gather(aux_b, 'row', axis=0, tiled=True)  53.8 us
    all_gather x2, waiting for transfers between devices, rates(): lax.all_gather(panel_sums, 'row', axis=0, tiled=True)  43.9 us
    all_gather x2, waiting for transfers between devices, rates(): col_block = lax.all_gather(dens_b, 'row', axis=1, tiled=True)  25.6 us
  transfers between devices with their start and end apart: 11, of which 11 were waited for; matrix products, arithmetic and copies ran while one was open for 16% of the time, Pallas kernels for 0%

profile of v1, /device:TPU:0, one launch (start us, length us, event | category | flops | bytes accessed | tf_op | source)
XLA Modules:
  0.0 678.9 jit_solution(6655149623970787362)
XLA Ops:
  7.2 4.0 fusion.11
  11.2 1.8 all_gather_reshape.6
  13.1 1.6 copy.52
  17.0 123.4 %all-gather.18.cloned.1.call-done = f32[8,512,512]{2,1,0:T(8,128)} async-done(((f32[1,512,512]{2,1,0:T(8,128)}), f32[8,512,512]{2,1,0:T(8,128)}) %all-gather.18.cloned.1.call-update) | async-done | bytes 8388624 | tf_op jit(solution)/shard_map/all_gather | solution.py:89
  140.4 5.5 reduce_sum.18
  145.9 3.3 convert_element_type.35
  149.2 2.6 reshape.105
  152.5 61.1 %all-gather.16.cloned.1.call-done = bf16[2,512,2048]{1,2,0:T(8,128)(2,1)} async-done(((bf16[2,512,256]{1,2,0:T(8,128)(2,1)}), bf16[2,512,2048]{1,2,0:T(8,128)(2,1)}) %all-gather.16.cloned.1.call-update) | async-done | bytes 4194320 | tf_op jit(solution)/shard_map/all_gather | solution.py:66
  213.6 6.3 copy.53
  219.9 10.5 %all-gather.14.cloned.1.call-done = bf16[2048,256]{1,0:T(8,128)(2,1)} async-done(((bf16[512,256]{1,0:T(8,128)(2,1)}), bf16[2048,256]{1,0:T(8,128)(2,1)}) %all-gather.14.cloned.1.call-update) | async-done | bytes 1048592 | tf_op jit(solution)/shard_map/all_gather | solution.py:31
  230.4 4.8 convolution_bitcast_fusion.4
  235.2 2.5 copy.54
  237.7 2.6 copy.55
  240.3 14.1 %all-gather.12.cloned.1.call-done = bf16[2,2048,256]{1,2,0:T(8,128)(2,1)} async-done(((bf16[2,512,256]{1,2,0:T(8,128)(2,1)}), bf16[2,2048,256]{1,2,0:T(8,128)(2,1)}) %all-gather.12.cloned.1.call-update) | async-done | bytes 2097168 | tf_op jit(solution)/shard_map/all_gather | solution.py:62
  254.4 4.1 fusion.26
  258.5 31.8 %all-gather.20.cloned.1.call-done = f32[2048,512]{1,0:T(8,128)} async-done(((f32[512,512]{1,0:T(8,128)}), f32[2048,512]{1,0:T(8,128)}) %all-gather.20.cloned.1.call-update) | async-done | bytes 4194320 | tf_op jit(solution)/shard_map/all_gather | solution.py:90
  290.3 5.4 copy.57
  295.7 2.0 convolution_bitcast_fusion.3
  297.7 2.2 convolution_bitcast_fusion.2
  303.0 1.7 broadcast_multiply_fusion
  304.7 22.1 %all-gather.26.cloned.1.call-done = bf16[2048,1024]{1,0:T(8,128)(2,1)} async-done(((bf16[512,1024]{1,0:T(8,128)(2,1)}), bf16[2048,1024]{1,0:T(8,128)(2,1)}) %all-gather.26.cloned.1.call-update) | async-done | bytes 4194320 | tf_op jit(solution)/shard_map/all_gather | solution.py:59
  326.8 5.8 fusion.94
  332.6 4.2 reshape.106
  336.8 5.0 multiply_subtract_fusion.1
  346.6 55.2 %all-gather.24.cloned.1.call-done = bf16[2,512,2048]{1,2,0:T(8,128)(2,1)} async-done(((bf16[2,512,256]{1,2,0:T(8,128)(2,1)}), bf16[2,512,2048]{1,2,0:T(8,128)(2,1)}) %all-gather.24.cloned.1.call-update) | async-done | bytes 4194320 | tf_op jit(solution)/shard_map/all_gather | solution.py:66
  401.8 6.3 copy.72
  408.1 4.3 fusion.29
  416.5 7.8 %add_subtract_fusion = (f32[512,4,2,128]{3,2,1,0:T(2,128)}, f32[512,4,2,128]{3,2,1,0:T(2,128)S(1)}) fusion(f32[512,2,128]{2,1,0:T(2,128)S(1)} %copy.76, f32[512,2,128]{2,1,0:T(2,128)S(1)} %copy.75, f32[512,4,128]{2,1,0:T(4,128)S(1)} %copy-done.12, f32[512,4,128]{2,1,0:T(4,128)S(1)} %copy-done.13, f32[4]{0:T(128)S(1)} %get-tuple-element.33, ...), kind=kLoop, calls=%fused_computation.11 | loop fusion | flops 5242880 | bytes 8388640 | tf_op jit(solution)/shard_map/sub | solution.py:109
  424.3 5.6 fusion.39
  429.9 3.8 fusion.91
  435.1 3.3 fusion.14
  438.4 3.1 all_gather_reshape.7
  442.3 2.6 reshape.109
  445.0 119.7 %all-gather.28.cloned.1.call-done = f32[8,512,512]{2,1,0:T(8,128)} async-done(((f32[1,512,512]{2,1,0:T(8,128)}), f32[8,512,512]{2,1,0:T(8,128)}) %all-gather.28.cloned.1.call-update) | async-done | bytes 8388624 | tf_op jit(solution)/shard_map/all_gather | solution.py:89
  564.7 5.5 reduce_sum.19
  570.2 5.3 fusion.41
  575.5 11.5 %all-gather.22.cloned.1.call-done = bf16[2,2048,256]{1,2,0:T(8,128)(2,1)} async-done(((bf16[2,512,256]{1,2,0:T(8,128)(2,1)}), bf16[2,2048,256]{1,2,0:T(8,128)(2,1)}) %all-gather.22.cloned.1.call-update) | async-done | bytes 2097168 | tf_op jit(solution)/shard_map/all_gather | solution.py:62
  587.0 4.2 fusion.23
  591.2 31.7 %all-gather.32.cloned.1.call-done = bf16[2048,1024]{1,0:T(8,128)(2,1)} async-done(((bf16[512,1024]{1,0:T(8,128)(2,1)}), bf16[2048,1024]{1,0:T(8,128)(2,1)}) %all-gather.32.cloned.1.call-update) | async-done | bytes 4194320 | tf_op jit(solution)/shard_map/all_gather | solution.py:59
  622.9 5.9 fusion.95
  628.9 4.4 copy.71
  633.3 4.0 multiply_subtract_fusion
  637.4 5.4 multiply_subtract_fusion.2
  642.8 4.6 fusion
  647.4 12.1 %all-gather.30.cloned.1.call-done = f32[2048,512]{1,0:T(8,128)} async-done(((f32[512,512]{1,0:T(8,128)}), f32[2048,512]{1,0:T(8,128)}) %all-gather.30.cloned.1.call-update) | async-done | bytes 4194320 | tf_op jit(solution)/shard_map/all_gather | solution.py:90
  659.6 5.5 copy.68
  665.0 2.2 convolution_bitcast_fusion
  667.2 1.9 convolution_bitcast_fusion.1
  (107 shorter events, 19.6 us)
Async XLA Ops:
  7.2 8.4 %copy-start = (bf16[512,2048]{1,0:T(8,128)(2,1)S(1)}, bf16[512,2048]{1,0:T(8,128)(2,1)}, u32[]{:S(2)}) copy-start(bf16[512,2048]{1,0:T(8,128)(2,1)} %param.12) | copy-start | bytes 6291460
  7.2 133.2 %all-gather.18.cloned.1.call-start = ((), (), s32[]{:S(2)}) async-start(), calls=%async_computation.3 | async-start | bytes 9437184 | tf_op jit(solution)/shard_map/all_gather | solution.py:89
  13.0 200.5 %all-gather.16.cloned.1.call-start = ((), (), s32[]{:S(2)}) async-start(), calls=%async_computation.2 | async-start | bytes 4718592 | tf_op jit(solution)/shard_map/all_gather | solution.py:66
  15.6 214.9 %all-gather.14.cloned.1.call-start = ((), (), s32[]{:S(2)}) async-start(), calls=%async_computation.1 | async-start | bytes 1310720 | tf_op jit(solution)/shard_map/all_gather | solution.py:31
  16.4 238.0 %all-gather.12.cloned.1.call-start = ((), (), s32[]{:S(2)}) async-start(), calls=%async_computation | async-start | bytes 2621440 | tf_op jit(solution)/shard_map/all_gather | solution.py:62
  17.0 273.4 %all-gather.20.cloned.1.call-start = ((), (), s32[]{:S(2)}) async-start(), calls=%async_computation.4 | async-start | bytes 5242880 | tf_op jit(solution)/shard_map/all_gather | solution.py:90
  145.9 180.9 %all-gather.26.cloned.1.call-start = ((), (), s32[]{:S(2)}) async-start(), calls=%async_computation.7 | async-start | bytes 5242880 | tf_op jit(solution)/shard_map/all_gather | solution.py:59
  151.9 249.9 %all-gather.24.cloned.1.call-start = ((), (), s32[]{:S(2)}) async-start(), calls=%async_computation.6 | async-start | bytes 4718592 | tf_op jit(solution)/shard_map/all_gather | solution.py:66
  258.5 37.2 %copy-start.19 = (s32[2,128]{1,0:T(2,128)S(1)}, s32[2,128]{1,0:T(2,128)}, u32[]{:S(2)}) copy-start(s32[2,128]{1,0:T(2,128)} %param.13) | copy-start | bytes 3076
  295.7 4.2 copy-start.17
  300.3 0.8 copy-start.8
  300.3 1.0 copy-start.10
  300.3 2.1 copy-start.22
  300.3 2.1 copy-start.23
  300.3 2.1 copy-start.24
  300.3 2.3 copy-start.18
  302.3 262.3 %all-gather.28.cloned.1.call-start = ((), (), s32[]{:S(2)}) async-start(), calls=%async_computation.8 | async-start | bytes 9437184 | tf_op jit(solution)/shard_map/all_gather | solution.py:89
  332.6 4.2 copy-start.20
  336.8 5.0 copy-start.14
  414.8 1.2 copy-start.12
  414.8 1.5 copy-start.13
  414.8 1.7 copy-start.15
  416.5 7.8 %copy-start.1 = (f32[512,4,2,128]{3,2,1,0:T(2,128)S(1)}, f32[512,4,2,128]{3,2,1,0:T(2,128)}, u32[]{:S(2)}) copy-start(f32[512,4,2,128]{3,2,1,0:T(2,128)} %param.11) | copy-start | bytes 6291460
  416.5 7.8 %copy-start.7 = (f32[512,4,2,128]{3,2,1,0:T(2,128)S(1)}, f32[512,4,2,128]{3,2,1,0:T(2,128)}, u32[]{:S(2)}) copy-start(f32[512,4,2,128]{3,2,1,0:T(2,128)} %multiply_subtract_fusion.1) | copy-start | bytes 6291460
  416.5 7.8 %copy-start.21 = (f32[4]{0:T(128)S(1)}, f32[4]{0:T(128)}, u32[]{:S(2)}) copy-start(f32[4]{0:T(128)} %param.16) | copy-start | bytes 52
  429.9 3.8 copy-start.4
  433.8 1.3 copy-start.2
  441.5 145.5 %all-gather.22.cloned.1.call-start = ((), (), s32[]{:S(2)}) async-start(), calls=%async_computation.5 | async-start | bytes 2621440 | tf_op jit(solution)/shard_map/all_gather | solution.py:62
  442.3 180.7 %all-gather.32.cloned.1.call-start = ((), (), s32[]{:S(2)}) async-start(), calls=%async_computation.10 | async-start | bytes 5242880 | tf_op jit(solution)/shard_map/all_gather | solution.py:59
  445.0 214.6 %all-gather.30.cloned.1.call-start = ((), (), s32[]{:S(2)}) async-start(), calls=%async_computation.9 | async-start | bytes 5242880 | tf_op jit(solution)/shard_map/all_gather | solution.py:90
  633.3 4.1 copy-start.3
  633.3 4.1 copy-start.6
  637.4 5.4 copy-start.5
  665.0 4.2 copy-start.16
  669.2 1.0 copy-start.9
  669.2 1.2 copy-start.11
Sparse Core Ops, SparseCore 0:
  13.2 127.1 all-gather.17
  142.6 70.9 all-gather.15
  215.1 15.2 all-gather.13
  231.8 22.5 all-gather.11
  255.8 34.4 all-gather.19
  292.3 34.4 all-gather.25
  329.0 72.7 all-gather.23
  441.7 122.9 all-gather.27
  566.3 20.7 all-gather.21
  588.4 34.4 all-gather.31
  625.1 34.4 all-gather.29
